TPU v7x, 32 devices: a whole 2x2x4 slice. The times are simulated.
32 devices in a mesh: dp: 8 (over y, x, core), seq: 4 (over z).
Axes of the slice: x: 2, y: 2, z: 4, core: 2. Of those that a mesh axis runs over, the one named last changes fastest.
Arguments:
- block_input: bfloat16 [16, 512, 2048], P('dp', 'seq'), may hold values from -12 to 12
- segment_ids: int32 [16, 512], P('dp'), may hold values from 0 to 3, never falling along the last dimension, each value on 1 to 256 neighbouring positions
- cotangent: bfloat16 [16, 512, 2048], P('dp', 'seq'), may hold values from -6 to 6
- attn_gain: float32 [2048], P(('dp', 'seq')), may hold values from 0.5 to 1.5
- qkv_weight: float32 [2048, 3072], P('dp', 'seq'), may hold values from -1 to 1
- out_weight: float32 [2048, 2048], P('seq', 'dp'), may hold values from -0.75 to 0.75
- mlp_gain: float32 [2048], P(('dp', 'seq')), may hold values from 0.5 to 1.5
- gate_up_weight: float32 [2048, 2, 8192], P('dp', None, 'seq'), may hold values from -0.125 to 0.125
- down_weight: float32 [8192, 2048], P('seq', 'dp'), may hold values from -0.125 to 0.125
- first_attn_gain: float32 [2048], P(('dp', 'seq')), may hold values from -30 to 30
- first_qkv: float32 [2048, 3072], P('dp', 'seq'), may hold values from -30 to 30
- first_out: float32 [2048, 2048], P('seq', 'dp'), may hold values from -30 to 30
- first_mlp_gain: float32 [2048], P(('dp', 'seq')), may hold values from -30 to 30
- first_gate_up: float32 [2048, 2, 8192], P('dp', None, 'seq'), may hold values from -30 to 30
- first_down: float32 [8192, 2048], P('seq', 'dp'), may hold values from -30 to 30
- second_attn_gain: float32 [2048], P(('dp', 'seq')), may hold values from 100 to 300000
- second_qkv: float32 [2048, 3072], P('dp', 'seq'), may hold values from 100 to 30000
- second_out: float32 [2048, 2048], P('seq', 'dp'), may hold values from 50 to 500
- second_mlp_gain: float32 [2048], P(('dp', 'seq')), may hold values from 50 to 500
- second_gate_up: float32 [2048, 2, 8192], P('dp', None, 'seq'), may hold values from 50 to 500
- second_down: float32 [8192, 2048], P('seq', 'dp'), may hold values from 50 to 500
Outputs:
- output: bfloat16 [16, 512, 2048], P('dp', 'seq')
- input_grad: bfloat16 [16, 512, 2048], P('dp', 'seq')
- grad_attn_gain: float32 [2048], P(('dp', 'seq'))
- grad_qkv: float32 [2048, 3072], P('dp', 'seq')
- grad_out: float32 [2048, 2048], P('seq', 'dp')
- grad_mlp_gain: float32 [2048], P(('dp', 'seq'))
- grad_gate_up: float32 [2048, 2, 8192], P('dp', None, 'seq')
- grad_down: float32 [8192, 2048], P('seq', 'dp')
- new_attn_gain: float32 [2048], P(('dp', 'seq'))
- new_qkv: float32 [2048, 3072], P('dp', 'seq')
- new_out: float32 [2048, 2048], P('seq', 'dp')
- new_mlp_gain: float32 [2048], P(('dp', 'seq'))
- new_gate_up: float32 [2048, 2, 8192], P('dp', None, 'seq')
- new_down: float32 [8192, 2048], P('seq', 'dp')
- new_first_attn_gain: float32 [2048], P(('dp', 'seq'))
- new_first_qkv: float32 [2048, 3072], P('dp', 'seq')
- new_first_out: float32 [2048, 2048], P('seq', 'dp')
- new_first_mlp_gain: float32 [2048], P(('dp', 'seq'))
- new_first_gate_up: float32 [2048, 2, 8192], P('dp', None, 'seq')
- new_first_down: float32 [8192, 2048], P('seq', 'dp')
- new_second_attn_gain: float32 [2048], P(('dp', 'seq'))
- new_second_qkv: float32 [2048, 3072], P('dp', 'seq')
- new_second_out: float32 [2048, 2048], P('seq', 'dp')
- new_second_mlp_gain: float32 [2048], P(('dp', 'seq'))
- new_second_gate_up: float32 [2048, 2, 8192], P('dp', None, 'seq')
- new_second_down: float32 [8192, 2048], P('seq', 'dp')
Inputs may be any that keep to these rules, and one draw needn't show every extreme that they name: `segment_ids`: in each sequence the numbers never fall, and each segment holds 1 to 256 consecutive positions, one of them exactly that many.
All inputs are finite; a program needn't handle non-finite values.
Results may differ from a plain program's by a relative error of at most 0.023.
Values may be sent and summed in bfloat16 or wider, within the bound.
A program may use at most 320 MiB of HBM per device.

v0:
```python
import jax
import jax.numpy as jnp
from jax import lax
from jax.sharding import PartitionSpec as P

HEADS = 32
KV_HEADS = 8
HEAD_DIM = 64
norm_eps = 1e-05
rope_base = 500000.0
beta_one = 0.9
beta_two = 0.95
learn_rate = 0.01
weight_decay = 0.1
adam_eps = 1e-08
step_count = 10.0
masked_score = -1e30


def segment_positions(segments):
    length_here = segments.shape[-1]
    earlier = (segments[..., None, :] < segments[..., :, None]).astype(jnp.int32)
    return jnp.arange(length_here, dtype=jnp.int32) - jnp.sum(earlier, axis=-1, dtype=jnp.int32)


def rope_tables(positions, head_size):
    half_size = head_size // 2
    inverse = rope_base ** (-2.0 * jnp.arange(half_size, dtype=jnp.float32) / head_size)
    angles = positions.astype(jnp.float32)[..., None] * inverse
    return (jnp.cos(angles), jnp.sin(angles))


def rotate(vectors, cosine, sine):
    half_size = vectors.shape[-1] // 2
    first_half = vectors[..., :half_size]
    second_half = vectors[..., half_size:]
    cos_wide = cosine[..., None, :]
    sin_wide = sine[..., None, :]
    return jnp.concatenate(
        [
            first_half * cos_wide - second_half * sin_wide,
            second_half * cos_wide + first_half * sin_wide,
        ],
        -1,
    )


def unrotate(vectors, cosine, sine):
    half_size = vectors.shape[-1] // 2
    first_half = vectors[..., :half_size]
    second_half = vectors[..., half_size:]
    cos_wide = cosine[..., None, :]
    sin_wide = sine[..., None, :]
    return jnp.concatenate(
        [
            first_half * cos_wide + second_half * sin_wide,
            second_half * cos_wide - first_half * sin_wide,
        ],
        -1,
    )


def rms_forward(values, gain_wide):
    inverse = lax.rsqrt(jnp.mean(values * values, axis=-1, keepdims=True) + norm_eps)
    scaled = values * inverse
    return (scaled, inverse, (scaled * gain_wide).astype(jnp.bfloat16))


def rms_backward(d_normed, scaled, inverse, gain_wide):
    d_scaled = d_normed * gain_wide
    d_values = inverse * (d_scaled - scaled * jnp.mean(d_scaled * scaled, axis=-1, keepdims=True))
    return (d_values, jnp.sum(d_normed * scaled, axis=0))


def adam_update(weight, grad, first, second):
    new_first = beta_one * first + (1.0 - beta_one) * grad
    new_second = beta_two * second + (1.0 - beta_two) * grad * grad
    first_hat = new_first / (1.0 - beta_one**step_count)
    second_hat = new_second / (1.0 - beta_two**step_count)
    new_weight = weight - learn_rate * (
        first_hat / (jnp.sqrt(second_hat) + adam_eps) + weight_decay * weight
    )
    return (new_weight, new_first, new_second)


def contract_rows(left, right):
    return lax.dot_general(
        left, right, (((0,), (0,)), ((), ())), preferred_element_type=jnp.float32
    )


def times_transpose(left, right):
    return lax.dot_general(
        left, right, (((1,), (1,)), ((), ())), preferred_element_type=jnp.float32
    )


def per_device(
    block_input,
    segment_ids,
    cotangent,
    attn_gain,
    qkv_weight,
    out_weight,
    mlp_gain,
    gate_up_weight,
    down_weight,
    first_attn_gain,
    first_qkv,
    first_out,
    first_mlp_gain,
    first_gate_up,
    first_down,
    second_attn_gain,
    second_qkv,
    second_out,
    second_mlp_gain,
    second_gate_up,
    second_down,
):
    seqs_here, local_len, width = block_input.shape
    full_len = segment_ids.shape[1]
    total_rows = seqs_here * full_len
    groups = HEADS // KV_HEADS
    slot_count = groups + 2
    kv_local = qkv_weight.shape[1] // (slot_count * HEAD_DIM)
    query_cols = kv_local * groups * HEAD_DIM
    unit_count = down_weight.shape[0]
    score_scale = HEAD_DIM ** (-0.5)
    local_rows = seqs_here * local_len
    gain_pair = jnp.stack([attn_gain, mlp_gain]).astype(jnp.bfloat16)
    gain_block = lax.all_gather(gain_pair, ("dp", "seq"), axis=1, tiled=True)
    gain_one = gain_block[0].astype(jnp.float32)
    gain_two = gain_block[1].astype(jnp.float32)
    local_input = block_input.reshape(local_rows, width).astype(jnp.float32)
    scaled_one, inverse_one, normed_here = rms_forward(local_input, gain_one)
    normed_one = lax.all_gather(
        normed_here.reshape(seqs_here, local_len, width), "seq", axis=1, tiled=True
    ).reshape(total_rows, width)
    qkv_cols = lax.all_gather(qkv_weight.astype(jnp.bfloat16), "dp", axis=0, tiled=True)
    out_rows = lax.all_gather(out_weight.astype(jnp.bfloat16), "dp", axis=1, tiled=True)
    gate_up_cols = lax.all_gather(
        gate_up_weight.astype(jnp.bfloat16).reshape(-1, 2 * unit_count), "dp", axis=0, tiled=True
    )
    cot_all = lax.all_gather(cotangent, "seq", axis=1, tiled=True)
    down_rows = lax.all_gather(down_weight.astype(jnp.bfloat16), "dp", axis=1, tiled=True)
    positions = segment_positions(segment_ids)
    cosine, sine = rope_tables(positions, HEAD_DIM)
    index_line = jnp.arange(full_len, dtype=jnp.int32)
    allowed = (segment_ids[:, :, None] == segment_ids[:, None, :]) & (
        index_line[None, None, :] <= index_line[None, :, None]
    )
    allowed = allowed[:, None, None, :, :]
    qkv = jnp.dot(normed_one, qkv_cols, preferred_element_type=jnp.float32)
    qkv = qkv.reshape(seqs_here, full_len, kv_local, slot_count, HEAD_DIM)
    query = qkv[:, :, :, :groups].reshape(seqs_here, full_len, kv_local * groups, HEAD_DIM)
    query_groups = (
        rotate(query, cosine, sine)
        .astype(jnp.bfloat16)
        .reshape(seqs_here, full_len, kv_local, groups, HEAD_DIM)
    )
    key16 = rotate(qkv[:, :, :, groups], cosine, sine).astype(jnp.bfloat16)
    value16 = qkv[:, :, :, groups + 1].astype(jnp.bfloat16)

    def masked_scores():
        raw_scores = (
            jnp.einsum("sqgjd,skgd->sgjqk", query_groups, key16, preferred_element_type=jnp.float32)
            * score_scale
        )
        return jnp.where(allowed, raw_scores, masked_score)

    scores = masked_scores()
    top_score = jnp.max(scores, axis=-1, keepdims=True)
    log_total = top_score + jnp.log(jnp.sum(jnp.exp(scores - top_score), axis=-1, keepdims=True))
    probs16 = jnp.exp(scores - log_total).astype(jnp.bfloat16)
    attended16 = jnp.einsum(
        "sgjqk,skgd->sqgjd", probs16, value16, preferred_element_type=jnp.float32
    )
    attended16 = attended16.reshape(total_rows, query_cols).astype(jnp.bfloat16)
    attn_part = jnp.dot(attended16, out_rows, preferred_element_type=jnp.float32)

    def to_local(part):
        return (
            lax.psum_scatter(
                part.astype(jnp.bfloat16).reshape(seqs_here, full_len, width),
                "seq",
                scatter_dimension=1,
                tiled=True,
            )
            .astype(jnp.float32)
            .reshape(local_rows, width)
        )

    resid = local_input + to_local(attn_part)
    scaled_two, inverse_two, normed_two_here = rms_forward(resid, gain_two)
    normed_two = lax.all_gather(
        normed_two_here.reshape(seqs_here, local_len, width), "seq", axis=1, tiled=True
    ).reshape(total_rows, width)
    gate_up = jnp.dot(normed_two, gate_up_cols, preferred_element_type=jnp.float32)
    gate_part = gate_up[:, :unit_count]
    up_part = gate_up[:, unit_count:]
    sigmoid_gate = jax.nn.sigmoid(gate_part)
    active = gate_part * sigmoid_gate
    hidden16 = (active * up_part).astype(jnp.bfloat16)
    down_part = jnp.dot(hidden16, down_rows, preferred_element_type=jnp.float32)
    output = (resid + to_local(down_part)).astype(jnp.bfloat16).reshape(block_input.shape)
    cot_rows = cot_all.reshape(total_rows, width)
    d_hidden = times_transpose(cot_rows, down_rows)
    d_gate = d_hidden * up_part * sigmoid_gate * (1.0 + gate_part * (1.0 - sigmoid_gate))
    d_up = d_hidden * active
    d_gate_up16 = jnp.concatenate([d_gate, d_up], 1).astype(jnp.bfloat16)
    d_normed_two = to_local(times_transpose(d_gate_up16, gate_up_cols))
    down_term = contract_rows(cot_rows, hidden16)
    gate_up_term = contract_rows(normed_two, d_gate_up16)
    down_sum = lax.psum_scatter(
        down_term.astype(jnp.bfloat16), "dp", scatter_dimension=0, tiled=True
    ).astype(jnp.float32)
    grad_gate_up = (
        lax.psum_scatter(gate_up_term.astype(jnp.bfloat16), "dp", scatter_dimension=0, tiled=True)
        .reshape(gate_up_weight.shape)
        .astype(jnp.float32)
    )
    grad_down = down_sum.T
    resid_part, gain_two_term = rms_backward(d_normed_two, scaled_two, inverse_two, gain_two)
    d_resid = cotangent.reshape(local_rows, width).astype(jnp.float32) + resid_part
    d_resid16 = lax.all_gather(
        d_resid.astype(jnp.bfloat16).reshape(seqs_here, local_len, width), "seq", axis=1, tiled=True
    ).reshape(total_rows, width)
    d_attended = times_transpose(d_resid16, out_rows).astype(jnp.bfloat16)
    d_attended = d_attended.reshape(seqs_here, full_len, kv_local, groups, HEAD_DIM)
    scores = masked_scores()
    probs = jnp.exp(scores - log_total)
    d_probs = jnp.einsum(
        "sqgjd,skgd->sgjqk", d_attended, value16, preferred_element_type=jnp.float32
    )
    delta = jnp.sum(probs * d_probs, axis=-1, keepdims=True)
    d_scores16 = (probs * (d_probs - delta) * score_scale).astype(jnp.bfloat16)
    d_query = jnp.einsum("sgjqk,skgd->sqgjd", d_scores16, key16, preferred_element_type=jnp.float32)
    d_key = jnp.einsum(
        "sgjqk,sqgjd->skgd", d_scores16, query_groups, preferred_element_type=jnp.float32
    )
    d_value = jnp.einsum(
        "sgjqk,sqgjd->skgd", probs16, d_attended, preferred_element_type=jnp.float32
    )
    d_query = unrotate(
        d_query.reshape(seqs_here, full_len, kv_local * groups, HEAD_DIM), cosine, sine
    )
    d_query = d_query.reshape(seqs_here, full_len, kv_local, groups, HEAD_DIM)
    d_key = unrotate(d_key, cosine, sine)
    d_qkv16 = jnp.concatenate([d_query, d_key[:, :, :, None], d_value[:, :, :, None]], 3)
    d_qkv16 = d_qkv16.reshape(total_rows, qkv_cols.shape[1]).astype(jnp.bfloat16)
    d_normed_one = to_local(times_transpose(d_qkv16, qkv_cols))
    qkv_term = contract_rows(normed_one, d_qkv16)
    out_term = contract_rows(d_resid16, attended16)
    grad_qkv = lax.psum_scatter(
        qkv_term.astype(jnp.bfloat16), "dp", scatter_dimension=0, tiled=True
    ).astype(jnp.float32)
    out_sum = lax.psum_scatter(
        out_term.astype(jnp.bfloat16), "dp", scatter_dimension=0, tiled=True
    ).astype(jnp.float32)
    grad_out = out_sum.T
    input_part, gain_one_term = rms_backward(d_normed_one, scaled_one, inverse_one, gain_one)
    input_grad = (d_resid + input_part).astype(jnp.bfloat16).reshape(block_input.shape)
    gain_grads = lax.psum_scatter(
        jnp.stack([gain_one_term, gain_two_term], 1), ("dp", "seq"), scatter_dimension=0, tiled=True
    )
    grad_gain_one = gain_grads[:, 0]
    grad_gain_two = gain_grads[:, 1]
    w_one, m_one, v_one = adam_update(attn_gain, grad_gain_one, first_attn_gain, second_attn_gain)
    w_qkv, m_qkv, v_qkv = adam_update(qkv_weight, grad_qkv, first_qkv, second_qkv)
    w_out, m_out, v_out = adam_update(out_weight, grad_out, first_out, second_out)
    w_two, m_two, v_two = adam_update(mlp_gain, grad_gain_two, first_mlp_gain, second_mlp_gain)
    w_gu, m_gu, v_gu = adam_update(gate_up_weight, grad_gate_up, first_gate_up, second_gate_up)
    w_down, m_down, v_down = adam_update(down_weight, grad_down, first_down, second_down)
    return (
        output,
        input_grad,
        grad_gain_one,
        grad_qkv,
        grad_out,
        grad_gain_two,
        grad_gate_up,
        grad_down,
        w_one,
        w_qkv,
        w_out,
        w_two,
        w_gu,
        w_down,
        m_one,
        m_qkv,
        m_out,
        m_two,
        m_gu,
        m_down,
        v_one,
        v_qkv,
        v_out,
        v_two,
        v_gu,
        v_down,
    )


def solution(mesh):
    in_specs = (
        P("dp", "seq", None),
        P("dp", None),
        P("dp", "seq", None),
        P(("dp", "seq")),
        P("dp", "seq"),
        P("seq", "dp"),
        P(("dp", "seq")),
        P("dp", None, "seq"),
        P("seq", "dp"),
        P(("dp", "seq")),
        P("dp", "seq"),
        P("seq", "dp"),
        P(("dp", "seq")),
        P("dp", None, "seq"),
        P("seq", "dp"),
        P(("dp", "seq")),
        P("dp", "seq"),
        P("seq", "dp"),
        P(("dp", "seq")),
        P("dp", None, "seq"),
        P("seq", "dp"),
    )
    out_specs = (
        P("dp", "seq", None),
        P("dp", "seq", None),
        P(("dp", "seq")),
        P("dp", "seq"),
        P("seq", "dp"),
        P(("dp", "seq")),
        P("dp", None, "seq"),
        P("seq", "dp"),
        P(("dp", "seq")),
        P("dp", "seq"),
        P("seq", "dp"),
        P(("dp", "seq")),
        P("dp", None, "seq"),
        P("seq", "dp"),
        P(("dp", "seq")),
        P("dp", "seq"),
        P("seq", "dp"),
        P(("dp", "seq")),
        P("dp", None, "seq"),
        P("seq", "dp"),
        P(("dp", "seq")),
        P("dp", "seq"),
        P("seq", "dp"),
        P(("dp", "seq")),
        P("dp", None, "seq"),
        P("seq", "dp"),
    )
    return jax.shard_map(
        per_device, mesh=mesh, in_specs=in_specs, out_specs=out_specs, check_vma=False
    )
```

profile of v0, /device:TPU:0, one launch (start us, length us, event | category | flops | bytes accessed | tf_op | source)
XLA Modules:
  0.0 1514.0 jit_solution(13102967327842110868)
XLA Ops:
  7.3 2.0 convert_element_type.162
  10.0 69.8 %all-gather = bf16[32,64,2]{1,2,0:T(2,128)(2,1)S(1)} all-gather(bf16[1,64,2]{1,2,0:T(2,128)(2,1)S(1)} %maximum_bitcast_fusion.4), channel_id=1, replica_groups=mesh['dp'=8,'seq'=4] {'dp','seq'}, dimensions={0}, use_global_device_ids=true | all-gather | bytes 8448 | tf_op jit(solution)/shard_map/all_gather | solution.py:132
  79.9 1.5 fusion.32
  81.5 2.5 fusion.29
  86.3 4.8 copy.86
  91.1 70.0 %all-gather.10.cloned.1.call-done = bf16[2,512,2048]{2,1,0:T(8,128)(2,1)} async-done(((bf16[2,128,2048]{2,1,0:T(8,128)(2,1)}), bf16[2,512,2048]{2,1,0:T(8,128)(2,1)}) %all-gather.10.cloned.1.call-update) | async-done | bytes 4194320 | tf_op jit(solution)/shard_map/all_gather | solution.py:137
  161.2 6.3 fusion.9
  169.2 7.4 fusion.5
  176.6 9.6 exponential_reduce_fusion
  186.2 10.3 fusion.35
  196.5 1.1 copy.88
  197.9 6.4 convolution_convert_fusion.2
  204.3 75.1 %reduce-scatter.12.cloned.1.call-done = bf16[2,128,2048]{2,1,0:T(8,128)(2,1)} async-done(((bf16[2,512,2048]{2,1,0:T(8,128)(2,1)}), bf16[2,128,2048]{2,1,0:T(8,128)(2,1)}) %reduce-scatter.12.cloned.1.call-update) | async-done | bytes 1048592 | tf_op jit(solution)/shard_map/reduce_scatter | solution.py:184
  279.4 1.6 multiply_reduce_fusion
  281.0 2.6 multiply_convert_fusion.3
  283.7 4.2 convert_element_type.174
  287.9 2.2 copy.122
  292.1 72.9 %all-gather.16.cloned.1.call-done = bf16[2,512,2048]{2,1,0:T(8,128)(2,1)} async-done(((bf16[2,128,2048]{2,1,0:T(8,128)(2,1)}), bf16[2,512,2048]{2,1,0:T(8,128)(2,1)}) %all-gather.16.cloned.1.call-update) | async-done | bytes 4194320 | tf_op jit(solution)/shard_map/all_gather | solution.py:196
  365.0 90.6 %all-gather.18.cloned.1.call-done = bf16[2048,4096]{1,0:T(8,128)(2,1)} async-done(((bf16[256,4096]{1,0:T(8,128)(2,1)}), bf16[2048,4096]{1,0:T(8,128)(2,1)}) %all-gather.18.cloned.1.call-update) | async-done | bytes 16777232 | tf_op jit(solution)/shard_map/all_gather | solution.py:142
  455.6 23.9 %fusion.71 = f32[1024,4096]{1,0:T(8,128)} fusion(bf16[1024,2048]{1,0:T(8,128)(2,1)} %bitcast.221, bf16[2048,4096]{1,0:T(8,128)(2,1)} %all-gather.18.cloned.1.call-done), kind=kOutput, calls=%fused_computation.139 | convolution fusion | flops 17179869184 | bytes 37748736 | tf_op jit(solution)/shard_map/dot_general | solution.py:199
  479.5 58.4 %all-gather.22.cloned.1.call-done = bf16[2,512,2048]{2,1,0:T(8,128)(2,1)} async-done(((bf16[2,128,2048]{2,1,0:T(8,128)(2,1)}), bf16[2,512,2048]{2,1,0:T(8,128)(2,1)}) %all-gather.22.cloned.1.call-update) | async-done | bytes 4194320 | tf_op jit(solution)/shard_map/all_gather | solution.py:145
  538.0 56.8 %all-gather.20.cloned.1.call-done = bf16[2048,2048]{1,0:T(8,128)(2,1)} async-done(((bf16[2048,256]{1,0:T(8,128)(2,1)}), bf16[2048,2048]{1,0:T(8,128)(2,1)}) %all-gather.20.cloned.1.call-update) | async-done | bytes 8388624 | tf_op jit(solution)/shard_map/all_gather | solution.py:146
  594.8 21.7 %multiply_convert_fusion.1 = (bf16[1024,2048]{1,0:T(8,128)(2,1)}, bf16[1024,2048]{1,0:T(8,128)(2,1)}, bf16[1024,2048]{1,0:T(8,128)(2,1)}) fusion(f32[1024,4096]{1,0:T(8,128)} %fusion.71, bf16[1024,2048]{1,0:T(8,128)(2,1)} %bitcast.223, bf16[2048,2048]{1,0:T(8,128)(2,1)} %all-gather.20.cloned.1.call-done), kind=kOutput, calls=%fused_computation.15 | convolution fusion | flops 8621391872 | bytes 41943040 | tf_op jit(solution)/shard_map/dot_general | solution.py:93
  616.5 23.8 %fusion.11 = bf16[1024,2048]{1,0:T(8,128)(2,1)} fusion(bf16[2048,4096]{1,0:T(8,128)(2,1)} %all-gather.18.cloned.1.call-done, bf16[1024,2048]{1,0:T(8,128)(2,1)} %get-tuple-element.129, bf16[1024,2048]{1,0:T(8,128)(2,1)} %get-tuple-element.128), kind=kOutput, calls=%fused_computation.26 | convolution fusion | flops 17198743552 | bytes 29360128 | tf_op jit(solution)/shard_map/dot_general | solution.py:93
  640.6 76.7 %reduce-scatter.16.cloned.1.call-done = bf16[2,128,2048]{2,1,0:T(8,128)(2,1)} async-done(((bf16[2,512,2048]{2,1,0:T(8,128)(2,1)}), bf16[2,128,2048]{2,1,0:T(8,128)(2,1)}) %reduce-scatter.16.cloned.1.call-update) | async-done | bytes 1048592 | tf_op jit(solution)/shard_map/reduce_scatter | solution.py:184
  717.3 2.0 fusion.28
  719.4 3.2 fusion.38
  722.7 81.3 %all-gather.24.cloned.1.call-done = bf16[2,512,2048]{2,1,0:T(8,128)(2,1)} async-done(((bf16[2,128,2048]{2,1,0:T(8,128)(2,1)}), bf16[2,512,2048]{2,1,0:T(8,128)(2,1)}) %all-gather.24.cloned.1.call-update) | async-done | bytes 4194320 | tf_op jit(solution)/shard_map/all_gather | solution.py:226
  804.0 6.2 convolution_convert_fusion.7
  810.2 4.6 reshape.347
  814.8 4.0 copy.90
  818.9 9.5 fusion.42
  828.4 24.6 %fusion.18 = f32[2,2,64,4,512]{4,2,3,1,0:T(8,128)} fusion(f32[2,2,512,512,4]{3,2,4,1,0:T(8,128)} %fusion.42, f32[2,2,512,512,4]{3,2,4,1,0:T(8,128)} %get-tuple-element.148, f32[2,2,4,512]{3,2,1,0:T(4,128)S(1)} %bitcast.215, pred[2,512,512]{1,2,0:T(8,128)(4,1)} %copy-done.10, bf16[2,512,2,32]{1,3,2,0:T(8,128)(2,1)S(1)} %get-tuple-element.140, ...), kind=kOutput, calls=%fused_computation.42 | convolution fusion | flops 583541248 | bytes 36470784 | tf_op jit(solution)/shard_map/sgjqk,skgd->sqgjd/dot_general | solution.py:238
  853.0 24.9 %fusion.36 = f32[2,512,2,64]{1,3,2,0:T(8,128)} fusion(f32[2,2,512,512,4]{3,2,4,1,0:T(8,128)} %fusion.42, f32[2,2,512,512,4]{3,2,4,1,0:T(8,128)} %get-tuple-element.148, f32[2,2,4,512]{3,2,1,0:T(4,128)S(1)} %bitcast.216, pred[2,512,512]{1,2,0:T(8,128)(4,1)} %copy-done.10, bf16[2,512,2,4,32]{1,4,3,2,0:T(8,128)(2,1)} %bitcast.201, ...), kind=kOutput, calls=%fused_computation.75 | convolution fusion | flops 585114112 | bytes 35684352 | tf_op jit(solution)/shard_map/sgjqk,sqgjd->skgd/dot_general | solution.py:239
  877.9 10.3 convolution_bitcast_fusion
  890.5 6.1 maximum_convert_fusion
  897.1 5.0 convolution_convert_fusion.3
  902.2 14.5 convert_bitcast_fusion
  916.8 6.2 convolution_convert_fusion.5
  923.1 7.9 convolution_convert_fusion.4
  931.1 14.0 convolution_convert_fusion.1
  945.2 32.4 %reduce-scatter.18.cloned.1.call-done = bf16[2,128,2048]{2,1,0:T(8,128)(2,1)} async-done(((bf16[2,512,2048]{2,1,0:T(8,128)(2,1)}), bf16[2,128,2048]{2,1,0:T(8,128)(2,1)}) %reduce-scatter.18.cloned.1.call-update) | async-done | bytes 1048592 | tf_op jit(solution)/shard_map/reduce_scatter | solution.py:184
  977.6 1.9 fusion.31
  979.6 1.3 copy.115
  981.0 25.4 %convolution_convert_fusion = bf16[2048,4096]{1,0:T(8,128)(2,1)} fusion(bf16[1024,2048]{1,0:T(8,128)(2,1)} %bitcast.222, bf16[1024,2048]{1,0:T(8,128)(2,1)} %get-tuple-element.129, bf16[1024,2048]{1,0:T(8,128)(2,1)} %get-tuple-element.128), kind=kOutput, calls=%fused_computation.9 | convolution fusion | flops 17205035008 | bytes 29360128 | tf_op jit(solution)/shard_map/dot_general | solution.py:87
  1006.4 2.2 copy.101
  1008.6 2.0 copy.98
  1010.7 2.0 copy.99
  1012.7 40.1 %reduce-scatter.26.cloned.1.call-done = bf16[256,2048]{0,1:T(8,128)(2,1)} async-done(((bf16[2048,2048]{0,1:T(8,128)(2,1)}), bf16[256,2048]{0,1:T(8,128)(2,1)}) %reduce-scatter.26.cloned.1.call-update) | async-done | bytes 1048592 | tf_op jit(solution)/shard_map/reduce_scatter | solution.py:215
  1052.8 6.9 multiply_subtract_fusion.1
  1059.6 37.5 %reduce-scatter.22.cloned.1.call-done = bf16[256,512]{1,0:T(8,128)(2,1)} async-done(((bf16[2048,512]{1,0:T(8,128)(2,1)}), bf16[256,512]{1,0:T(8,128)(2,1)}) %reduce-scatter.22.cloned.1.call-update) | async-done | bytes 262160 | tf_op jit(solution)/shard_map/reduce_scatter | solution.py:258
  1097.2 2.9 multiply_subtract_fusion.4
  1100.1 2.0 copy.103
  1102.1 2.0 copy.104
  1104.2 2.0 copy.105
  1107.0 2.1 copy.102
  1109.1 37.4 %reduce-scatter.20.cloned.1.call-done = bf16[256,768]{1,0:T(8,128)(2,1)} async-done(((bf16[2048,768]{1,0:T(8,128)(2,1)}), bf16[256,768]{1,0:T(8,128)(2,1)}) %reduce-scatter.20.cloned.1.call-update) | async-done | bytes 393232 | tf_op jit(solution)/shard_map/reduce_scatter | solution.py:255
  1146.5 3.5 multiply_subtract_fusion.3
  1150.1 75.4 %reduce-scatter.14.cloned.1.call-done = bf16[2,128,2048]{2,1,0:T(8,128)(2,1)} async-done(((bf16[2,512,2048]{2,1,0:T(8,128)(2,1)}), bf16[2,128,2048]{2,1,0:T(8,128)(2,1)}) %reduce-scatter.14.cloned.1.call-update) | async-done | bytes 1048592 | tf_op jit(solution)/shard_map/reduce_scatter | solution.py:184
  1225.5 4.9 fusion.24
  1230.4 135.3 %reduce-scatter.28.cloned.1.call-done = f32[64,2]{1,0:T(8,128)} async-done(((f32[2048,2]{1,0:T(8,128)}), f32[64,2]{1,0:T(8,128)}) %reduce-scatter.28.cloned.1.call-update) | async-done | bytes 528
  1367.9 113.8 %reduce-scatter.24.cloned.1.call-done = bf16[256,4096]{1,0:T(8,128)(2,1)} async-done(((bf16[2048,4096]{1,0:T(8,128)(2,1)}), bf16[256,4096]{1,0:T(8,128)(2,1)}) %reduce-scatter.24.cloned.1.call-update) | async-done | bytes 2097168 | tf_op jit(solution)/shard_map/reduce_scatter | solution.py:219
  1481.7 6.6 reshape.336
  1488.3 18.9 %multiply_subtract_fusion = (f32[256,2,2048]{2,1,0:T(2,128)}, f32[256,2,2048]{2,1,0:T(2,128)}, f32[256,2,2048]{2,1,0:T(2,128)}) fusion(f32[256,2,2048]{2,1,0:T(2,128)} %param.28, f32[256,2,2048]{2,1,0:T(2,128)} %reshape.336, f32[256,2,2048]{2,1,0:T(2,128)} %param.34, f32[256,2,2048]{2,1,0:T(2,128)} %param.40), kind=kLoop, calls=%fused_computation.24 | loop fusion | flops 15728640 | bytes 29360128 | tf_op jit(solution)/shard_map/sub | solution.py:80
  (138 shorter events, 13.5 us)
Async XLA Ops:
  7.2 76.8 %copy-start.11 = (f32[512,256]{1,0:T(8,128)S(1)}, f32[512,256]{1,0:T(8,128)}, u32[]{:S(2)}) copy-start(f32[512,256]{1,0:T(8,128)} %param.26) | copy-start | bytes 1572868
  7.2 77.8 %copy-start.21 = (s32[2,512]{1,0:T(2,128)S(1)}, s32[2,512]{1,0:T(2,128)}, u32[]{:S(2)}) copy-start(s32[2,512]{1,0:T(2,128)} %param.22) | copy-start | bytes 12292
  7.2 79.1 %all-gather.12.cloned.1.call-start = ((), (), s32[]{:S(2)}) async-start(), calls=%async_computation.10 | async-start | bytes 3538944 | tf_op jit(solution)/shard_map/all_gather | solution.py:140
  9.3 151.9 %all-gather.10.cloned.1.call-start = ((), (), s32[]{:S(2)}) async-start(), calls=%async_computation.9 | async-start | bytes 5242880 | tf_op jit(solution)/shard_map/all_gather | solution.py:137
  81.4 3.8 copy-start.22
  81.5 3.8 copy-start.19
  84.0 113.9 %all-gather.14.cloned.1.call-start = ((), (), s32[]{:S(2)}) async-start(), calls=%async_computation.11 | async-start | bytes 2359296 | tf_op jit(solution)/shard_map/all_gather | solution.py:141
  84.8 194.6 %reduce-scatter.12.cloned.1.call-start = ((), (), s32[]{:S(2)}) async-start(), calls=%async_computation.12 | async-start | bytes 5242880 | tf_op jit(solution)/shard_map/reduce_scatter | solution.py:184
  85.7 100.4 %copy-start.10 = (pred[2,512,512]{1,2,0:T(8,128)(4,1)}, pred[2,512,512]{1,2,0:T(8,128)(4,1)S(1)}, u32[]{:S(2)}) copy-start(pred[2,512,512]{1,2,0:T(8,128)(4,1)S(1)} %compare_and_fusion) | copy-start | bytes 1572868
  86.3 81.5 %copy-start.4 = (f32[2,512,32]{1,2,0:T(8,128)}, f32[2,512,32]{1,2,0:T(8,128)S(1)}, u32[]{:S(2)}) copy-start(f32[2,512,32]{1,2,0:T(8,128)S(1)} %get-tuple-element.145) | copy-start | bytes 393220
  86.3 81.5 %copy-start.6 = (f32[2,512,32]{1,2,0:T(8,128)}, f32[2,512,32]{1,2,0:T(8,128)S(1)}, u32[]{:S(2)}) copy-start(f32[2,512,32]{1,2,0:T(8,128)S(1)} %get-tuple-element.146) | copy-start | bytes 393220
  167.5 1.7 copy-start.9
  169.2 7.4 copy-start.17
  169.2 7.4 copy-start.18
  197.9 6.4 copy-start.14
  204.2 75.1 %copy-start = (bf16[2,128,2048]{2,1,0:T(8,128)(2,1)S(1)}, bf16[2,128,2048]{2,1,0:T(8,128)(2,1)}, u32[]{:S(2)}) copy-start(bf16[2,128,2048]{2,1,0:T(8,128)(2,1)} %param.21) | copy-start | bytes 3145732
  204.3 160.8 %all-gather.16.cloned.1.call-start = ((), (), s32[]{:S(2)}) async-start(), calls=%async_computation.13 | async-start | bytes 5242880 | tf_op jit(solution)/shard_map/all_gather | solution.py:196
  283.7 172.0 %all-gather.18.cloned.1.call-start = ((), (), s32[]{:S(2)}) async-start(), calls=%async_computation.14 | async-start | bytes 18874368 | tf_op jit(solution)/shard_map/all_gather | solution.py:142
  287.9 3.1 copy-start.3
  290.2 247.8 %all-gather.22.cloned.1.call-start = ((), (), s32[]{:S(2)}) async-start(), calls=%async_computation.17 | async-start | bytes 5242880 | tf_op jit(solution)/shard_map/all_gather | solution.py:145
  290.9 303.9 %all-gather.20.cloned.1.call-start = ((), (), s32[]{:S(2)}) async-start(), calls=%async_computation.15 | async-start | bytes 9437184 | tf_op jit(solution)/shard_map/all_gather | solution.py:146
  292.1 425.2 %reduce-scatter.16.cloned.1.call-start = ((), (), s32[]{:S(2)}) async-start(), calls=%async_computation.18 | async-start | bytes 5242880 | tf_op jit(solution)/shard_map/reduce_scatter | solution.py:184
  640.3 77.0 %copy-start.1 = (bf16[2,128,2048]{2,1,0:T(8,128)(2,1)S(1)}, bf16[2,128,2048]{2,1,0:T(8,128)(2,1)}, u32[]{:S(2)}) copy-start(bf16[2,128,2048]{2,1,0:T(8,128)(2,1)} %reduce-scatter.12.cloned.1.call-done) | copy-start | bytes 3145732
  640.3 79.0 %copy-start.2 = (bf16[2,128,2048]{2,1,0:T(8,128)(2,1)S(1)}, bf16[2,128,2048]{2,1,0:T(8,128)(2,1)}, u32[]{:S(2)}) copy-start(bf16[2,128,2048]{2,1,0:T(8,128)(2,1)} %param.23) | copy-start | bytes 3145732
  640.4 163.6 %all-gather.24.cloned.1.call-start = ((), (), s32[]{:S(2)}) async-start(), calls=%async_computation.19 | async-start | bytes 5242880 | tf_op jit(solution)/shard_map/all_gather | solution.py:226
  722.6 255.0 %reduce-scatter.18.cloned.1.call-start = ((), (), s32[]{:S(2)}) async-start(), calls=%async_computation.20 | async-start | bytes 5242880 | tf_op jit(solution)/shard_map/reduce_scatter | solution.py:184
  877.9 10.4 copy-start.5
  877.9 10.4 copy-start.7
  877.9 10.3 copy-start.12
  888.2 1.6 copy-start.16
  889.9 7.2 copy-start.8
  897.1 5.1 copy-start.13
  902.2 150.6 %reduce-scatter.26.cloned.1.call-start = ((), (), s32[]{:S(2)}) async-start(), calls=%async_computation.24 | async-start | bytes 9437184 | tf_op jit(solution)/shard_map/reduce_scatter | solution.py:215
  916.8 180.4 %reduce-scatter.22.cloned.1.call-start = ((), (), s32[]{:S(2)}) async-start(), calls=%async_computation.22 | async-start | bytes 2359296 | tf_op jit(solution)/shard_map/reduce_scatter | solution.py:258
  923.0 223.5 %reduce-scatter.20.cloned.1.call-start = ((), (), s32[]{:S(2)}) async-start(), calls=%async_computation.21 | async-start | bytes 3538944 | tf_op jit(solution)/shard_map/reduce_scatter | solution.py:255
  931.0 294.5 %reduce-scatter.14.cloned.1.call-start = ((), (), s32[]{:S(2)}) async-start(), calls=%async_computation.16 | async-start | bytes 5242880 | tf_op jit(solution)/shard_map/reduce_scatter | solution.py:184
  945.1 32.5 %copy-start.20 = (f32[1,2048]{1,0:T(1,128)S(1)}, f32[1,2048]{1,0:T(1,128)}, u32[]{:S(2)}) copy-start(f32[1,2048]{1,0:T(1,128)} %copy-done.19) | copy-start | bytes 24580
  945.1 32.5 %copy-start.23 = (f32[2,128]{1,0:T(2,128)S(1)}, f32[2,128]{1,0:T(2,128)}, u32[]{:S(2)}) copy-start(f32[2,128]{1,0:T(2,128)} %copy-done.22) | copy-start | bytes 3076
  945.1 420.6 %reduce-scatter.28.cloned.1.call-start = ((), (), s32[]{:S(2)}) async-start(), calls=%async_computation.25 | async-start | bytes 1081344
  981.0 500.8 %reduce-scatter.24.cloned.1.call-start = ((), (), s32[]{:S(2)}) async-start(), calls=%async_computation.23 | async-start | bytes 18874368 | tf_op jit(solution)/shard_map/reduce_scatter | solution.py:219
  1097.2 9.0 copy-start.15
  1150.0 216.7 %copy-start.26 = (f32[64]{0:T(128)S(1)}, f32[64]{0:T(128)}, u32[]{:S(2)}) copy-start(f32[64]{0:T(128)} %param.27) | copy-start | bytes 772
  1150.0 216.7 %copy-start.28 = (f32[64]{0:T(128)S(1)}, f32[64]{0:T(128)}, u32[]{:S(2)}) copy-start(f32[64]{0:T(128)} %param.33) | copy-start | bytes 772
  1150.0 216.7 %copy-start.29 = (f32[64]{0:T(128)S(1)}, f32[64]{0:T(128)}, u32[]{:S(2)}) copy-start(f32[64]{0:T(128)} %param.39) | copy-start | bytes 772
  1150.0 217.3 %copy-start.27 = (f32[64]{0:T(128)S(1)}, f32[64]{0:T(128)}, u32[]{:S(2)}) copy-start(f32[64]{0:T(128)} %param.24) | copy-start | bytes 772
  1150.1 217.3 %copy-start.30 = (f32[64]{0:T(128)S(1)}, f32[64]{0:T(128)}, u32[]{:S(2)}) copy-start(f32[64]{0:T(128)} %param.30) | copy-start | bytes 772
  1150.1 217.3 %copy-start.31 = (f32[64]{0:T(128)S(1)}, f32[64]{0:T(128)}, u32[]{:S(2)}) copy-start(f32[64]{0:T(128)} %param.36) | copy-start | bytes 772
  1366.7 140.5 %copy-start.24 = (f32[64,1]{0,1:T(1,128)}, f32[64,1]{0,1:T(1,128)S(1)}, u32[]{:S(2)}) copy-start(f32[64,1]{0,1:T(1,128)S(1)} %copy.120) | copy-start | bytes 772
  1366.8 140.4 %copy-start.25 = (f32[64,1]{0,1:T(1,128)}, f32[64,1]{0,1:T(1,128)S(1)}, u32[]{:S(2)}) copy-start(f32[64,1]{0,1:T(1,128)S(1)} %copy.119) | copy-start | bytes 772
Sparse Core Ops, SparseCore 0:
  10.5 34.9 all-gather.11
  84.1 76.9 all-gather.9
  163.6 26.5 all-gather.13
  204.4 74.9 reduce-scatter.11
  283.8 81.2 all-gather.15
  367.4 88.2 all-gather.17
  457.2 80.7 all-gather.21
  540.4 54.3 all-gather.19
  640.5 76.7 reduce-scatter.15
  722.7 81.2 all-gather.23
  902.3 75.2 reduce-scatter.17
  980.9 71.7 reduce-scatter.25
  1056.1 41.0 reduce-scatter.21
  1100.4 46.0 reduce-scatter.19
  1148.6 76.7 reduce-scatter.13
  1228.1 137.5 reduce-scatter.27
  1369.1 112.5 reduce-scatter.23
where the time goes:
time: 1520 us; the launch traced here: 1510 us
  waiting for transfers between devices  1050 us (69%)
  matrix products  248 us (16%)
  other arithmetic  81.3 us (5%)
  blocking collectives  69.8 us (5%)
  local copies, waits for them, and re-layouts  43.9 us (3%)
    reduce_scatter x4, waiting for transfers between devices, to_local(): lax.psum_scatter(part.astype(jnp.bfloat16).reshape(seqs_here, full_len, w...  260 us
    unnamed x18, waiting for transfers between devices  136 us
    reduce_scatter x1, waiting for transfers between devices, per_device(): lax.psum_scatter(gate_up_term.astype(jnp.bfloat16), 'dp', scatter_dimensi...  114 us
    all_gather x1, waiting for transfers between devices, per_device(): lax.all_gather(gate_up_weight.astype(jnp.bfloat16).reshape(-1, 2 * unit_c...  90.6 us
    all_gather x1, waiting for transfers between devices, per_device(): lax.all_gather(d_resid.astype(jnp.bfloat16).reshape(seqs_here, local_len,...  81.3 us
    all_gather x1, waiting for transfers between devices, per_device(): lax.all_gather(normed_two_here.reshape(seqs_here, local_len, width), 'seq...  72.9 us
    all_gather x1, waiting for transfers between devices, per_device(): lax.all_gather(normed_here.reshape(seqs_here, local_len, width), 'seq', a...  70 us
    all_gather x1, blocking collectives, per_device(): gain_block = lax.all_gather(gain_pair, ('dp', 'seq'), axis=1, tiled=True)  69.8 us
  transfers between devices with their start and end apart: 17, of which 15 were waited for; matrix products, arithmetic and copies ran while one was open for 12% of the time, Pallas kernels for 0%

commit v1 on v0

--- a/solution.py
+++ b/solution.py
@@ -139,9 +139,11 @@
     ).reshape(total_rows, width)
     qkv_cols = lax.all_gather(qkv_weight.astype(jnp.bfloat16), "dp", axis=0, tiled=True)
     out_rows = lax.all_gather(out_weight.astype(jnp.bfloat16), "dp", axis=1, tiled=True)
-    gate_up_cols = lax.all_gather(
-        gate_up_weight.astype(jnp.bfloat16).reshape(-1, 2 * unit_count), "dp", axis=0, tiled=True
-    )
+    own = gate_up_weight.astype(jnp.bfloat16).reshape(-1, 2 * unit_count)
+    count = lax.axis_size("dp")
+    shards = jnp.stack([own for _ in range(count)])
+    shards = lax.all_to_all(shards, "dp", split_axis=0, concat_axis=0)
+    gate_up_cols = jnp.concatenate(shards, axis=0)
     cot_all = lax.all_gather(cotangent, "seq", axis=1, tiled=True)
     down_rows = lax.all_gather(down_weight.astype(jnp.bfloat16), "dp", axis=1, tiled=True)
     positions = segment_positions(segment_ids)

time: 1520 us -> 1450 us (0.954)
  waiting for transfers between devices: 1050 us -> 978 us
    all_to_all x0 -> x1, waiting for transfers between devices: none -> 203 us  [per_device(): shards = lax.all_to_all(shards, 'dp', split_axis=0, concat_axis=0)]
    all_gather x1 -> x0, waiting for transfers between devices: 90.6 us -> none  [per_device(): lax.all_gather(gate_up_weight.astype(jnp.bfloat16).reshape(-1, 2 * unit_c...]
    all_gather x1, waiting for transfers between devices: 72.9 us -> 0.01 us  [per_device(): lax.all_gather(normed_two_here.reshape(seqs_here, local_len, width), 'seq...]
    all_gather x1, waiting for transfers between devices: 58.4 us -> 0.01 us  [per_device(): cot_all = lax.all_gather(cotangent, 'seq', axis=1, tiled=True)]
    all_gather x1, waiting for transfers between devices: 56.8 us -> 0.01 us  [per_device(): lax.all_gather(down_weight.astype(jnp.bfloat16), 'dp', axis=1, tiled=True)]
    unnamed x18 -> x17, waiting for transfers between devices: 136 us -> 136 us
  transfers between devices with their start and end apart: 17 -> 17, of which waited for: 15 -> 12; matrix products, arithmetic and copies ran while one was open for 12% -> 13% of each run, Pallas kernels for 0% -> 0%
where the time goes in v1:
time: 1450 us
  waiting for transfers between devices  978 us (67%)
  matrix products  248 us (17%)
  other arithmetic  81.3 us (6%)
  blocking collectives  69.8 us (5%)
  local copies, waits for them, and re-layouts  49.1 us (3%)
  between operations  14.8 us (1%)
    reduce_scatter x4, waiting for transfers between devices, to_local(): lax.psum_scatter(part.astype(jnp.bfloat16).reshape(seqs_here, full_len, w...  259 us
    all_to_all x1, waiting for transfers between devices, per_device(): shards = lax.all_to_all(shards, 'dp', split_axis=0, concat_axis=0)  203 us
    unnamed x17, waiting for transfers between devices  136 us
    reduce_scatter x1, waiting for transfers between devices, per_device(): lax.psum_scatter(gate_up_term.astype(jnp.bfloat16), 'dp', scatter_dimensi...  114 us
    all_gather x1, waiting for transfers between devices, per_device(): lax.all_gather(d_resid.astype(jnp.bfloat16).reshape(seqs_here, local_len,...  81.3 us
    all_gather x1, waiting for transfers between devices, per_device(): lax.all_gather(normed_here.reshape(seqs_here, local_len, width), 'seq', a...  70 us
    all_gather x1, blocking collectives, per_device(): gain_block = lax.all_gather(gain_pair, ('dp', 'seq'), axis=1, tiled=True)  69.8 us
    dot_general x4, matrix products, times_transpose(): lax.dot_general(left, right, (((1,), (1,)), ((), ())), preferred_element_...  56.8 us
  transfers between devices with their start and end apart: 17, of which 12 were waited for; matrix products, arithmetic and copies ran while one was open for 13% of the time, Pallas kernels for 0%

profile of v1, /device:TPU:0, one launch (start us, length us, event | category | flops | bytes accessed | tf_op | source)
XLA Modules:
  0.0 1447.9 jit_solution(8882844299108043412)
XLA Ops:
  7.3 2.0 convert_element_type.162
  10.0 69.8 %all-gather = bf16[32,64,2]{1,2,0:T(2,128)(2,1)S(1)} all-gather(bf16[1,64,2]{1,2,0:T(2,128)(2,1)S(1)} %maximum_bitcast_fusion.4), channel_id=1, replica_groups=mesh['dp'=8,'seq'=4] {'dp','seq'}, dimensions={0}, use_global_device_ids=true | all-gather | bytes 8448 | tf_op jit(solution)/shard_map/all_gather | solution.py:132
  79.9 1.5 fusion.32
  81.5 2.5 fusion.29
  86.3 4.8 copy.86
  91.1 70.0 %all-gather.9.cloned.1.call-done = bf16[2,512,2048]{2,1,0:T(8,128)(2,1)} async-done(((bf16[2,128,2048]{2,1,0:T(8,128)(2,1)}), bf16[2,512,2048]{2,1,0:T(8,128)(2,1)}) %all-gather.9.cloned.1.call-update) | async-done | bytes 4194320 | tf_op jit(solution)/shard_map/all_gather | solution.py:137
  161.2 6.3 fusion.9
  169.2 7.4 fusion.5
  176.6 9.6 exponential_reduce_fusion
  186.2 10.3 fusion.35
  196.5 1.1 copy.88
  197.9 6.4 convolution_convert_fusion.2
  204.7 74.7 %reduce-scatter.12.cloned.1.call-done = bf16[2,128,2048]{2,1,0:T(8,128)(2,1)} async-done(((bf16[2,512,2048]{2,1,0:T(8,128)(2,1)}), bf16[2,128,2048]{2,1,0:T(8,128)(2,1)}) %reduce-scatter.12.cloned.1.call-update) | async-done | bytes 1048592 | tf_op jit(solution)/shard_map/reduce_scatter | solution.py:186
  279.4 1.6 multiply_reduce_fusion
  281.0 2.6 multiply_convert_fusion.3
  284.2 4.2 convert_element_type.174
  289.3 6.5 stack.27
  295.9 5.9 all-to-all-start
  301.8 1.1 convert_element_type.176
  303.0 202.6 %all-to-all-done = bf16[8,256,4096]{2,1,0:T(8,128)(2,1)} async-done(((bf16[8,256,4096]{2,1,0:T(8,128)(2,1)}), bf16[8,256,4096]{2,1,0:T(8,128)(2,1)}, u32[]{:S(2)}, u32[]{:S(2)}) %all-to-all-start) | async-done | bytes 16777248 | tf_op jit(solution)/shard_map/all_to_all | solution.py:145
  505.6 23.4 %fusion.71 = f32[1024,4096]{1,0:T(8,128)} fusion(bf16[1024,2048]{1,0:T(8,128)(2,1)} %bitcast.222, bf16[2048,4096]{1,0:T(8,128)(2,1)} %bitcast.25), kind=kOutput, calls=%fused_computation.139 | convolution fusion | flops 17179869184 | bytes 37748736 | tf_op jit(solution)/shard_map/dot_general | solution.py:201
  529.0 21.8 %multiply_convert_fusion.1 = (bf16[1024,2048]{1,0:T(8,128)(2,1)}, bf16[1024,2048]{1,0:T(8,128)(2,1)}, bf16[1024,2048]{1,0:T(8,128)(2,1)}) fusion(f32[1024,4096]{1,0:T(8,128)} %fusion.71, bf16[1024,2048]{1,0:T(8,128)(2,1)} %bitcast.224, bf16[2048,2048]{1,0:T(8,128)(2,1)} %all-gather.17.cloned.1.call-done), kind=kOutput, calls=%fused_computation.15 | convolution fusion | flops 8621391872 | bytes 41943040 | tf_op jit(solution)/shard_map/dot_general | solution.py:93
  550.8 23.8 %fusion.11 = bf16[1024,2048]{1,0:T(8,128)(2,1)} fusion(bf16[2048,4096]{1,0:T(8,128)(2,1)} %bitcast.25, bf16[1024,2048]{1,0:T(8,128)(2,1)} %get-tuple-element.129, bf16[1024,2048]{1,0:T(8,128)(2,1)} %get-tuple-element.128), kind=kOutput, calls=%fused_computation.26 | convolution fusion | flops 17198743552 | bytes 29360128 | tf_op jit(solution)/shard_map/dot_general | solution.py:93
  574.8 76.1 %reduce-scatter.16.cloned.1.call-done = bf16[2,128,2048]{2,1,0:T(8,128)(2,1)} async-done(((bf16[2,512,2048]{2,1,0:T(8,128)(2,1)}), bf16[2,128,2048]{2,1,0:T(8,128)(2,1)}) %reduce-scatter.16.cloned.1.call-update) | async-done | bytes 1048592 | tf_op jit(solution)/shard_map/reduce_scatter | solution.py:186
  650.9 2.0 fusion.28
  653.0 3.2 fusion.38
  656.3 81.3 %all-gather.21.cloned.1.call-done = bf16[2,512,2048]{2,1,0:T(8,128)(2,1)} async-done(((bf16[2,128,2048]{2,1,0:T(8,128)(2,1)}), bf16[2,512,2048]{2,1,0:T(8,128)(2,1)}) %all-gather.21.cloned.1.call-update) | async-done | bytes 4194320 | tf_op jit(solution)/shard_map/all_gather | solution.py:228
  737.6 6.2 convolution_convert_fusion.7
  743.8 4.6 reshape.349
  748.5 4.0 copy.90
  752.5 9.5 fusion.42
  762.0 24.6 %fusion.18 = f32[2,2,64,4,512]{4,2,3,1,0:T(8,128)} fusion(f32[2,2,512,512,4]{3,2,4,1,0:T(8,128)} %fusion.42, f32[2,2,512,512,4]{3,2,4,1,0:T(8,128)} %get-tuple-element.148, f32[2,2,4,512]{3,2,1,0:T(4,128)S(1)} %bitcast.216, pred[2,512,512]{1,2,0:T(8,128)(4,1)} %copy-done.10, bf16[2,512,2,32]{1,3,2,0:T(8,128)(2,1)S(1)} %copy-done.22, ...), kind=kOutput, calls=%fused_computation.42 | convolution fusion | flops 583541248 | bytes 36470784 | tf_op jit(solution)/shard_map/sgjqk,skgd->sqgjd/dot_general | solution.py:240
  786.7 24.9 %fusion.36 = f32[2,512,2,64]{1,3,2,0:T(8,128)} fusion(f32[2,2,512,512,4]{3,2,4,1,0:T(8,128)} %fusion.42, f32[2,2,512,512,4]{3,2,4,1,0:T(8,128)} %get-tuple-element.148, f32[2,2,4,512]{3,2,1,0:T(4,128)S(1)} %bitcast.217, pred[2,512,512]{1,2,0:T(8,128)(4,1)} %copy-done.10, bf16[2,512,2,4,32]{1,4,3,2,0:T(8,128)(2,1)} %bitcast.202, ...), kind=kOutput, calls=%fused_computation.75 | convolution fusion | flops 585114112 | bytes 35684352 | tf_op jit(solution)/shard_map/sgjqk,sqgjd->skgd/dot_general | solution.py:241
  811.6 10.3 convolution_bitcast_fusion
  822.4 1.1 copy.92
  824.2 6.1 maximum_convert_fusion
  830.8 5.0 convolution_convert_fusion.3
  835.9 14.5 %convert_bitcast_fusion = bf16[2048,2048]{0,1:T(8,128)(2,1)} fusion(bf16[1024,2048]{1,0:T(8,128)(2,1)} %get-tuple-element.130, bf16[1024,2048]{1,0:T(8,128)(2,1)} %bitcast.225), kind=kOutput, calls=%fused_computation.13 | convolution fusion | flops 8594128896 | bytes 16777216 | tf_op jit(solution)/shard_map/dot_general | solution.py:87
  850.5 6.2 convolution_convert_fusion.5
  856.8 7.9 convolution_convert_fusion.4
  864.8 14.0 convolution_convert_fusion.1
  878.9 32.4 %reduce-scatter.18.cloned.1.call-done = bf16[2,128,2048]{2,1,0:T(8,128)(2,1)} async-done(((bf16[2,512,2048]{2,1,0:T(8,128)(2,1)}), bf16[2,128,2048]{2,1,0:T(8,128)(2,1)}) %reduce-scatter.18.cloned.1.call-update) | async-done | bytes 1048592 | tf_op jit(solution)/shard_map/reduce_scatter | solution.py:186
  911.3 1.9 fusion.31
  913.3 1.3 copy.115
  914.7 25.4 %convolution_convert_fusion = bf16[2048,4096]{1,0:T(8,128)(2,1)} fusion(bf16[1024,2048]{1,0:T(8,128)(2,1)} %bitcast.223, bf16[1024,2048]{1,0:T(8,128)(2,1)} %get-tuple-element.129, bf16[1024,2048]{1,0:T(8,128)(2,1)} %get-tuple-element.128), kind=kOutput, calls=%fused_computation.9 | convolution fusion | flops 17205035008 | bytes 29360128 | tf_op jit(solution)/shard_map/dot_general | solution.py:87
  940.1 2.2 copy.101
  942.3 2.0 copy.98
  944.4 2.0 copy.99
  946.4 40.2 %reduce-scatter.26.cloned.1.call-done = bf16[256,2048]{0,1:T(8,128)(2,1)} async-done(((bf16[2048,2048]{0,1:T(8,128)(2,1)}), bf16[256,2048]{0,1:T(8,128)(2,1)}) %reduce-scatter.26.cloned.1.call-update) | async-done | bytes 1048592 | tf_op jit(solution)/shard_map/reduce_scatter | solution.py:217
  986.6 6.9 multiply_subtract_fusion.1
  993.5 37.4 %reduce-scatter.22.cloned.1.call-done = bf16[256,512]{1,0:T(8,128)(2,1)} async-done(((bf16[2048,512]{1,0:T(8,128)(2,1)}), bf16[256,512]{1,0:T(8,128)(2,1)}) %reduce-scatter.22.cloned.1.call-update) | async-done | bytes 262160 | tf_op jit(solution)/shard_map/reduce_scatter | solution.py:260
  1030.9 2.9 multiply_subtract_fusion.4
  1033.8 2.0 copy.103
  1035.8 2.0 copy.104
  1037.8 2.0 copy.105
  1040.7 2.1 copy.102
  1042.8 37.6 %reduce-scatter.20.cloned.1.call-done = bf16[256,768]{1,0:T(8,128)(2,1)} async-done(((bf16[2048,768]{1,0:T(8,128)(2,1)}), bf16[256,768]{1,0:T(8,128)(2,1)}) %reduce-scatter.20.cloned.1.call-update) | async-done | bytes 393232 | tf_op jit(solution)/shard_map/reduce_scatter | solution.py:257
  1080.4 3.5 multiply_subtract_fusion.3
  1083.9 75.4 %reduce-scatter.14.cloned.1.call-done = bf16[2,128,2048]{2,1,0:T(8,128)(2,1)} async-done(((bf16[2,512,2048]{2,1,0:T(8,128)(2,1)}), bf16[2,128,2048]{2,1,0:T(8,128)(2,1)}) %reduce-scatter.14.cloned.1.call-update) | async-done | bytes 1048592 | tf_op jit(solution)/shard_map/reduce_scatter | solution.py:186
  1159.3 4.9 fusion.24
  1164.2 135.3 %reduce-scatter.28.cloned.1.call-done = f32[64,2]{1,0:T(8,128)} async-done(((f32[2048,2]{1,0:T(8,128)}), f32[64,2]{1,0:T(8,128)}) %reduce-scatter.28.cloned.1.call-update) | async-done | bytes 528
  1301.7 114.0 %reduce-scatter.24.cloned.1.call-done = bf16[256,4096]{1,0:T(8,128)(2,1)} async-done(((bf16[2048,4096]{1,0:T(8,128)(2,1)}), bf16[256,4096]{1,0:T(8,128)(2,1)}) %reduce-scatter.24.cloned.1.call-update) | async-done | bytes 2097168 | tf_op jit(solution)/shard_map/reduce_scatter | solution.py:221
  1415.7 6.6 reshape.338
  1422.2 18.9 %multiply_subtract_fusion = (f32[256,2,2048]{2,1,0:T(2,128)}, f32[256,2,2048]{2,1,0:T(2,128)}, f32[256,2,2048]{2,1,0:T(2,128)}) fusion(f32[256,2,2048]{2,1,0:T(2,128)} %param.28, f32[256,2,2048]{2,1,0:T(2,128)} %reshape.338, f32[256,2,2048]{2,1,0:T(2,128)} %param.34, f32[256,2,2048]{2,1,0:T(2,128)} %param.40), kind=kLoop, calls=%fused_computation.24 | loop fusion | flops 15728640 | bytes 29360128 | tf_op jit(solution)/shard_map/sub | solution.py:80
  (146 shorter events, 12.4 us)
Async XLA Ops:
  7.2 76.8 %copy-start.11 = (f32[512,256]{1,0:T(8,128)S(1)}, f32[512,256]{1,0:T(8,128)}, u32[]{:S(2)}) copy-start(f32[512,256]{1,0:T(8,128)} %param.26) | copy-start | bytes 1572868
  7.2 77.8 %copy-start.25 = (s32[2,512]{1,0:T(2,128)S(1)}, s32[2,512]{1,0:T(2,128)}, u32[]{:S(2)}) copy-start(s32[2,512]{1,0:T(2,128)} %param.22) | copy-start | bytes 12292
  7.2 79.1 %all-gather.11.cloned.1.call-start = ((), (), s32[]{:S(2)}) async-start(), calls=%async_computation.11 | async-start | bytes 3538944 | tf_op jit(solution)/shard_map/all_gather | solution.py:140
  9.3 151.9 %all-gather.9.cloned.1.call-start = ((), (), s32[]{:S(2)}) async-start(), calls=%async_computation.10 | async-start | bytes 5242880 | tf_op jit(solution)/shard_map/all_gather | solution.py:137
  81.4 3.8 copy-start.26
  81.5 3.8 copy-start.23
  84.0 113.9 %all-gather.13.cloned.1.call-start = ((), (), s32[]{:S(2)}) async-start(), calls=%async_computation.12 | async-start | bytes 2359296 | tf_op jit(solution)/shard_map/all_gather | solution.py:141
  84.8 194.6 %reduce-scatter.12.cloned.1.call-start = ((), (), s32[]{:S(2)}) async-start(), calls=%async_computation.13 | async-start | bytes 5242880 | tf_op jit(solution)/shard_map/reduce_scatter | solution.py:186
  85.7 100.4 %copy-start.10 = (pred[2,512,512]{1,2,0:T(8,128)(4,1)}, pred[2,512,512]{1,2,0:T(8,128)(4,1)S(1)}, u32[]{:S(2)}) copy-start(pred[2,512,512]{1,2,0:T(8,128)(4,1)S(1)} %compare_and_fusion) | copy-start | bytes 1572868
  86.3 81.6 %copy-start.4 = (f32[2,512,32]{1,2,0:T(8,128)}, f32[2,512,32]{1,2,0:T(8,128)S(1)}, u32[]{:S(2)}) copy-start(f32[2,512,32]{1,2,0:T(8,128)S(1)} %get-tuple-element.145) | copy-start | bytes 393220
  86.3 81.6 %copy-start.6 = (f32[2,512,32]{1,2,0:T(8,128)}, f32[2,512,32]{1,2,0:T(8,128)S(1)}, u32[]{:S(2)}) copy-start(f32[2,512,32]{1,2,0:T(8,128)S(1)} %get-tuple-element.146) | copy-start | bytes 393220
  167.5 1.7 copy-start.9
  167.6 8.9 copy-start.19
  167.7 8.9 copy-start.21
  169.2 7.4 copy-start.17
  169.2 7.4 copy-start.18
  197.9 6.4 copy-start.14
  204.3 75.1 %copy-start = (bf16[2,128,2048]{2,1,0:T(8,128)(2,1)S(1)}, bf16[2,128,2048]{2,1,0:T(8,128)(2,1)}, u32[]{:S(2)}) copy-start(bf16[2,128,2048]{2,1,0:T(8,128)(2,1)} %param.21) | copy-start | bytes 3145732
  204.3 301.3 %all-gather.15.cloned.1.call-start = ((), (), s32[]{:S(2)}) async-start(), calls=%async_computation.14 | async-start | bytes 5242880 | tf_op jit(solution)/shard_map/all_gather | solution.py:198
  283.7 245.3 %all-gather.19.cloned.1.call-start = ((), (), s32[]{:S(2)}) async-start(), calls=%async_computation.17 | async-start | bytes 5242880 | tf_op jit(solution)/shard_map/all_gather | solution.py:147
  295.9 5.9 copy-start.3
  295.9 209.7 %all-to-all-start = ((bf16[8,256,4096]{2,1,0:T(8,128)(2,1)}), bf16[8,256,4096]{2,1,0:T(8,128)(2,1)}, u32[]{:S(2)}, u32[]{:S(2)}) async-start(bf16[8,256,4096]{2,1,0:T(8,128)(2,1)} %stack.27), calls=%async_computation.1 | async-start | bytes 33554432 | tf_op jit(solution)/shard_map/all_to_all | solution.py:145
  301.8 227.2 %all-gather.17.cloned.1.call-start = ((), (), s32[]{:S(2)}) async-start(), calls=%async_computation.15 | async-start | bytes 9437184 | tf_op jit(solution)/shard_map/all_gather | solution.py:148
  302.9 348.0 %reduce-scatter.16.cloned.1.call-start = ((), (), s32[]{:S(2)}) async-start(), calls=%async_computation.18 | async-start | bytes 5242880 | tf_op jit(solution)/shard_map/reduce_scatter | solution.py:186
  574.6 76.4 %copy-start.1 = (bf16[2,128,2048]{2,1,0:T(8,128)(2,1)S(1)}, bf16[2,128,2048]{2,1,0:T(8,128)(2,1)}, u32[]{:S(2)}) copy-start(bf16[2,128,2048]{2,1,0:T(8,128)(2,1)} %reduce-scatter.12.cloned.1.call-done) | copy-start | bytes 3145732
  574.6 78.4 %copy-start.2 = (bf16[2,128,2048]{2,1,0:T(8,128)(2,1)S(1)}, bf16[2,128,2048]{2,1,0:T(8,128)(2,1)}, u32[]{:S(2)}) copy-start(bf16[2,128,2048]{2,1,0:T(8,128)(2,1)} %param.23) | copy-start | bytes 3145732
  574.6 163.0 %all-gather.21.cloned.1.call-start = ((), (), s32[]{:S(2)}) async-start(), calls=%async_computation.19 | async-start | bytes 5242880 | tf_op jit(solution)/shard_map/all_gather | solution.py:228
  656.2 255.1 %reduce-scatter.18.cloned.1.call-start = ((), (), s32[]{:S(2)}) async-start(), calls=%async_computation.20 | async-start | bytes 5242880 | tf_op jit(solution)/shard_map/reduce_scatter | solution.py:186
  752.5 9.5 copy-start.20
  752.5 9.5 copy-start.22
  811.6 10.4 copy-start.5
  811.6 10.4 copy-start.7
  811.6 10.3 copy-start.12
  821.9 1.6 copy-start.16
  823.6 7.2 copy-start.8
  830.8 5.1 copy-start.13
  835.9 150.7 %reduce-scatter.26.cloned.1.call-start = ((), (), s32[]{:S(2)}) async-start(), calls=%async_computation.24 | async-start | bytes 9437184 | tf_op jit(solution)/shard_map/reduce_scatter | solution.py:217
  850.5 180.4 %reduce-scatter.22.cloned.1.call-start = ((), (), s32[]{:S(2)}) async-start(), calls=%async_computation.22 | async-start | bytes 2359296 | tf_op jit(solution)/shard_map/reduce_scatter | solution.py:260
  856.8 223.6 %reduce-scatter.20.cloned.1.call-start = ((), (), s32[]{:S(2)}) async-start(), calls=%async_computation.21 | async-start | bytes 3538944 | tf_op jit(solution)/shard_map/reduce_scatter | solution.py:257
  864.7 294.6 %reduce-scatter.14.cloned.1.call-start = ((), (), s32[]{:S(2)}) async-start(), calls=%async_computation.16 | async-start | bytes 5242880 | tf_op jit(solution)/shard_map/reduce_scatter | solution.py:186
  878.8 32.5 %copy-start.24 = (f32[1,2048]{1,0:T(1,128)S(1)}, f32[1,2048]{1,0:T(1,128)}, u32[]{:S(2)}) copy-start(f32[1,2048]{1,0:T(1,128)} %copy-done.23) | copy-start | bytes 24580
  878.8 32.5 %copy-start.27 = (f32[2,128]{1,0:T(2,128)S(1)}, f32[2,128]{1,0:T(2,128)}, u32[]{:S(2)}) copy-start(f32[2,128]{1,0:T(2,128)} %copy-done.26) | copy-start | bytes 3076
  878.8 420.7 %reduce-scatter.28.cloned.1.call-start = ((), (), s32[]{:S(2)}) async-start(), calls=%async_computation.25 | async-start | bytes 1081344
  914.6 501.1 %reduce-scatter.24.cloned.1.call-start = ((), (), s32[]{:S(2)}) async-start(), calls=%async_computation.23 | async-start | bytes 18874368 | tf_op jit(solution)/shard_map/reduce_scatter | solution.py:221
  1030.9 9.0 copy-start.15
  1083.9 216.7 %copy-start.30 = (f32[64]{0:T(128)S(1)}, f32[64]{0:T(128)}, u32[]{:S(2)}) copy-start(f32[64]{0:T(128)} %param.27) | copy-start | bytes 772
  1083.9 216.7 %copy-start.32 = (f32[64]{0:T(128)S(1)}, f32[64]{0:T(128)}, u32[]{:S(2)}) copy-start(f32[64]{0:T(128)} %param.33) | copy-start | bytes 772
  1083.9 216.7 %copy-start.33 = (f32[64]{0:T(128)S(1)}, f32[64]{0:T(128)}, u32[]{:S(2)}) copy-start(f32[64]{0:T(128)} %param.39) | copy-start | bytes 772
  1083.9 217.3 %copy-start.31 = (f32[64]{0:T(128)S(1)}, f32[64]{0:T(128)}, u32[]{:S(2)}) copy-start(f32[64]{0:T(128)} %param.24) | copy-start | bytes 772
  1083.9 217.2 %copy-start.34 = (f32[64]{0:T(128)S(1)}, f32[64]{0:T(128)}, u32[]{:S(2)}) copy-start(f32[64]{0:T(128)} %param.30) | copy-start | bytes 772
  1083.9 217.2 %copy-start.35 = (f32[64]{0:T(128)S(1)}, f32[64]{0:T(128)}, u32[]{:S(2)}) copy-start(f32[64]{0:T(128)} %param.36) | copy-start | bytes 772
  1300.5 140.7 %copy-start.28 = (f32[64,1]{0,1:T(1,128)}, f32[64,1]{0,1:T(1,128)S(1)}, u32[]{:S(2)}) copy-start(f32[64,1]{0,1:T(1,128)S(1)} %copy.120) | copy-start | bytes 772
  1300.6 140.6 %copy-start.29 = (f32[64,1]{0,1:T(1,128)}, f32[64,1]{0,1:T(1,128)S(1)}, u32[]{:S(2)}) copy-start(f32[64,1]{0,1:T(1,128)S(1)} %copy.119) | copy-start | bytes 772
Sparse Core Ops, SparseCore 0:
  10.5 34.9 all-gather.10
  84.1 76.9 all-gather.8
  163.6 26.5 all-gather.12
  204.4 74.9 reduce-scatter.11
  283.8 81.2 all-gather.14
  366.5 79.2 all-gather.18
  448.2 74.7 all-gather.16
  574.7 76.1 reduce-scatter.15
  656.3 81.2 all-gather.20
  836.0 75.2 reduce-scatter.17
  914.8 71.7 reduce-scatter.25
  989.7 41.0 reduce-scatter.21
  1034.2 46.0 reduce-scatter.19
  1082.5 76.7 reduce-scatter.13
  1162.0 137.4 reduce-scatter.27
  1302.9 112.6 reduce-scatter.23
